TPU v7x, 32 devices: a whole 2x2x4 slice. The times are simulated.
32 devices in a mesh: groups: 2 (over y), range: 8 (over z, x), sub: 2 (over core).
Axes of the slice: x: 2, y: 2, z: 4, core: 2. Of those that a mesh axis runs over, the one named last changes fastest.
Arguments:
- samples: float32 [2, 1024, 32, 128], P(None, ('groups', 'range', 'sub')), parts along dimension 1, may hold values from -6 to 6
- beam_weights: float32 [32, 8, 2, 64, 128], P(('groups', 'range'), None, None, None, 'sub'), parts along dimension 0, may hold values from -0.25 to 0.25
- subarrays: int32 [32, 8, 64], P(('groups', 'range', 'sub')), parts along dimension 0, may hold values from 0 to 511, as said below
- training: int32 [64], P(('groups', 'range', 'sub')), parts along dimension 0, may hold values 0 or 1
Outputs:
- covariance: float32 [32, 8, 64, 128], P(('groups', 'range', 'sub')), parts along dimension 0
- filtered: float32 [2, 128, 64, 128], P(None, None, ('groups', 'range', 'sub')), parts along dimension 2
- energy: float32 [256], P('groups'), parts along dimension 0
There are 2 independent parts, one for each index of `groups`. A program takes and returns all parts, laid end to end along the dimension named above; each array names one. Nothing has to cross between parts.
Inputs may be any that keep to these rules, and one draw needn't show every extreme that they name: `subarrays`: in each gate block the 512 indices are all 512 channels, each once.
All inputs are finite; a program needn't handle non-finite values. No bound on the sum of `training` on one device may be relied on, other than what follows from the above.
Results may differ from a plain program's by a relative error of at most 0.0003.
Values sent between devices are 32-bit elements; how exact they have to be, the bound alone decides.
A program may use at most 64 MiB of HBM per device.

v0:
```python
import jax
import jax.numpy as jnp
from jax import lax
from jax.sharding import PartitionSpec as P

GB = 2
loading = 0.05


def block_terms(snaps, chosen, weights, masked, factor):
    highest = lax.Precision.HIGHEST
    picked = jnp.take(snaps, chosen, axis=1)
    real_part = picked[0]
    imag_part = picked[1]
    real_masked = real_part * masked
    imag_masked = imag_part * masked
    cov_real = (
        jnp.einsum("snx,smx->snm", real_masked, real_part, precision=highest)
        + jnp.einsum("snx,smx->snm", imag_masked, imag_part, precision=highest)
    ) * factor
    cov_imag = (
        jnp.einsum("snx,smx->snm", imag_masked, real_part, precision=highest)
        - jnp.einsum("snx,smx->snm", real_masked, imag_part, precision=highest)
    ) * factor
    w_real = weights[:, 0]
    w_imag = weights[:, 1]
    out_real = jnp.einsum("snk,snx->kx", w_real, real_part, precision=highest) + jnp.einsum(
        "snk,snx->kx", w_imag, imag_part, precision=highest
    )
    out_imag = jnp.einsum("snk,snx->kx", w_real, imag_part, precision=highest) - jnp.einsum(
        "snk,snx->kx", w_imag, real_part, precision=highest
    )
    prod_real = jnp.einsum("snm,smk->snk", cov_real, w_real, precision=highest) - jnp.einsum(
        "snm,smk->snk", cov_imag, w_imag, precision=highest
    )
    prod_imag = jnp.einsum("snm,smk->snk", cov_real, w_imag, precision=highest) + jnp.einsum(
        "snm,smk->snk", cov_imag, w_real, precision=highest
    )
    quadratic = jnp.sum(w_real * prod_real + w_imag * prod_imag, axis=(0, 1))
    inverse = 1.0 / jnp.sqrt(quadratic + loading)
    filtered = jnp.stack([out_real * inverse[:, None], out_imag * inverse[:, None]])
    energy = jnp.sum(out_real * out_real + out_imag * out_imag, axis=1)
    covariance = jnp.concatenate([cov_real, cov_imag], axis=-1)
    return (covariance, filtered, energy)


def body(samples, beam_weights, subarrays, training):
    range_count = lax.axis_size("range")
    core_count = lax.axis_size("sub")
    parts_iq, chan_dev, all_gates, pulses = samples.shape
    gate_dev = all_gates // (range_count * core_count)
    channels = chan_dev * range_count * core_count
    blocks_dev = gate_dev // GB
    spread = samples.reshape(parts_iq, 1, 1, chan_dev, range_count, core_count, gate_dev, pulses)
    turned = lax.all_to_all(
        lax.all_to_all(spread, "range", split_axis=4, concat_axis=1, tiled=True),
        "sub",
        split_axis=5,
        concat_axis=2,
        tiled=True,
    )
    local_data = turned.reshape(parts_iq, channels, blocks_dev, GB * pulses).transpose(2, 0, 1, 3)
    mine = lax.all_to_all(beam_weights, "sub", split_axis=0, concat_axis=4, tiled=True)
    gates_on = training.astype(jnp.float32).reshape(blocks_dev, GB)
    masked = jnp.repeat(gates_on, pulses, axis=1)
    factor = 1.0 / (GB * pulses)
    covs, filts, energies = jax.vmap(block_terms, in_axes=(0, 0, 0, 0, None))(
        local_data, subarrays, mine, masked, factor
    )
    beams = filts.shape[2]
    filtered = filts.reshape(blocks_dev, parts_iq, beams, GB, pulses).transpose(1, 2, 0, 3, 4)
    filtered = filtered.reshape(parts_iq, beams, gate_dev, pulses)
    total = lax.psum(jnp.sum(energies, axis=0), ("range", "sub"))
    energy = total / (all_gates * pulses)
    return (covs, filtered, energy)


def solution(mesh):
    placed = (
        P(None, ("groups", "range", "sub"), None, None),
        P(("groups", "range"), None, None, None, "sub"),
        P(("groups", "range", "sub"), None, None),
        P(("groups", "range", "sub")),
    )
    return jax.shard_map(
        body,
        mesh=mesh,
        in_specs=placed,
        out_specs=(
            P(("groups", "range", "sub"), None, None, None),
            P(None, None, ("groups", "range", "sub"), None),
            P("groups"),
        ),
        check_vma=False,
    )
```

profile of v0, /device:TPU:0, one launch (start us, length us, event | category | flops | bytes accessed | tf_op | source)
XLA Modules:
  0.0 92.5 jit_solution(9004139148378862796)
XLA Ops:
  0.6 2.5 %reshape.157 = f32[2,1,65536]{2,1,0:T(1,128)} reshape(f32[2,8,2,64,64]{4,3,2,1,0:T(8,128)} %param.5) | data formatting | bytes 1048576
  3.2 3.5 %all-to-all-start.2 = ((f32[2,1,65536]{2,1,0:T(1,128)}), f32[2,1,65536]{2,1,0:T(1,128)S(1)}, u32[]{:S(2)}, u32[]{:S(2)}) async-start(f32[2,1,65536]{2,1,0:T(1,128)} %reshape.157), calls=%async_computation.2 | async-start | bytes 1048576 | tf_op jit(solution)/shard_map/all_to_all | solution.py:63
  6.7 1.6 %copy.24 = f32[2,1,1,32,8,2,2,128]{7,6,3,5,0,2,1,4:T(2,128)} copy(f32[2,1,1,32,8,2,2,128]{7,6,5,4,3,0,2,1:T(2,128)S(1)} %bitcast.103) | data formatting | bytes 2097152 | tf_op jit(solution)/shard_map/reshape | solution.py:54
  8.2 0.2 all-to-all-done.2
  8.4 7.4 %all-to-all-start = ((f32[2,1,1,32,8,2,2,128]{7,6,3,5,0,2,1,4:T(2,128)}), f32[2,1,1,32,8,2,2,128]{7,6,3,5,0,2,1,4:T(2,128)S(1)}, u32[]{:S(2)}, u32[]{:S(2)}) async-start(f32[2,1,1,32,8,2,2,128]{7,6,3,5,0,2,1,4:T(2,128)} %copy.24), calls=%async_computation | async-start | bytes 2097152 | tf_op jit(solution)/shard_map/all_to_all | solution.py:56
  15.9 0.5 broadcast.75
  16.4 2.3 %reduce.5 = f32[2,65536]{1,0:T(2,128)S(1)} reduce(f32[2,1,65536]{2,1,0:T(1,128)S(1)} %all-to-all-done.2, f32[]{:T(128)} %broadcast.75), dimensions={1}, to_apply=%all_to_all.44.reduce_sub_computation | reduce | bytes 1048580 | tf_op jit(solution)/shard_map/all_to_all | solution.py:63
  18.8 0.6 reshape.158
  19.4 1.9 %copy.29 = f32[1,8,2,64,2,64]{5,4,3,1,2,0:T(2,128)} copy(f32[1,8,2,64,2,64]{5,3,2,1,4,0:T(8,128)S(1)} %bitcast.98) | data formatting | bytes 1048576 | tf_op jit(solution)/shard_map/all_to_all | solution.py:63
  21.2 1.8 %all_to_all.47 = f32[1,8,2,64,128]{4,3,1,2,0:T(8,128)S(1)} reshape(f32[1,8,2,64,2,64]{5,4,3,1,2,0:T(2,128)} %copy.29) | data formatting | bytes 1048576 | tf_op jit(solution)/shard_map/all_to_all | solution.py:63
  23.1 18.9 %all-to-all-done = f32[2,1,1,32,8,2,2,128]{7,6,3,5,0,2,1,4:T(2,128)S(1)} async-done(((f32[2,1,1,32,8,2,2,128]{7,6,3,5,0,2,1,4:T(2,128)}), f32[2,1,1,32,8,2,2,128]{7,6,3,5,0,2,1,4:T(2,128)S(1)}, u32[]{:S(2)}, u32[]{:S(2)}) %all-to-all-start) | async-done | bytes 1048608 | tf_op jit(solution)/shard_map/all_to_all | solution.py:56
  42.1 4.6 %all_to_all.51 = f32[2,8,1,32,1,2,2,128]{7,6,3,1,0,4,2,5:T(2,128)S(1)} all-to-all(f32[2,8,1,32,1,2,2,128]{7,6,3,1,0,4,2,5:T(2,128)S(1)} %copy.25), channel_id=1, replica_groups=mesh['groups'=2,'range'=8,'sub'=2] {'sub'}, dimensions={5} | all-to-all | bytes 2097152 | tf_op jit(solution)/shard_map/all_to_all | solution.py:55
  46.8 0.8 copy.27
  47.6 2.3 %gather_fusion = f32[512,2,256]{2,1,0:T(2,128)S(1)} fusion(f32[1,2,512,256]{3,1,2,0:T(2,128)S(1)} %copy.27, s32[512]{0:T(512)S(1)} %reshape.147), kind=kCustom, calls=%fused_computation | custom fusion | bytes 2101248 | tf_op jit(solution)/shard_map/vmap(jit(_take))/gather | solution.py:12
  50.1 0.1 broadcast_select_fusion
  50.2 1.0 %convolution_bitcast_fusion.2 = f32[256,128]{1,0:T(8,128)S(1)} fusion(f32[1,2,8,64,256]{4,3,2,1,0:T(8,128)S(1)} %broadcast_select_fusion, f32[1,8,2,64,128]{4,3,1,2,0:T(8,128)S(1)} %all_to_all.47), kind=kOutput, calls=%fused_computation.13 | convolution fusion | flops 201326592 | bytes 917504 | tf_op jit(solution)/shard_map/vmap(snk,snx->kx)/dot_general | solution.py:27
  51.2 1.0 %convolution_bitcast_fusion = f32[256,128]{1,0:T(8,128)S(1)} fusion(f32[1,2,8,64,256]{4,3,2,1,0:T(8,128)S(1)} %broadcast_select_fusion, f32[1,8,2,64,128]{4,3,1,2,0:T(8,128)S(1)} %all_to_all.47), kind=kOutput, calls=%fused_computation.11 | convolution fusion | flops 201326592 | bytes 917504 | tf_op jit(solution)/shard_map/vmap(snk,snx->kx)/dot_general | solution.py:30
  52.2 0.6 fusion.12
  52.9 0.6 fusion.2
  53.5 0.4 fusion.19
  53.9 0.4 fusion.18
  54.3 0.6 fusion.8
  54.9 1.0 %fusion.6 = f32[256,128]{1,0:T(8,128)S(1)} fusion(f32[256,128]{1,0:T(8,128)S(1)} %convolution_bitcast_fusion.2, f32[1,2,8,64,256]{4,3,2,1,0:T(8,128)S(1)} %broadcast_select_fusion, f32[1,8,2,64,128]{4,3,1,2,0:T(8,128)S(1)} %all_to_all.47), kind=kOutput, calls=%fused_computation.15 | convolution fusion | flops 201359360 | bytes 1048576 | tf_op jit(solution)/shard_map/vmap(snk,snx->kx)/dot_general | solution.py:27
  55.9 0.6 fusion.3
  56.5 0.4 fusion
  56.9 0.4 fusion.5
  57.4 1.0 %add_reduce_fusion = (f32[128]{0:T(128)S(1)}, f32[256,128]{1,0:T(8,128)S(1)}, f32[256,128]{1,0:T(8,128)S(1)}) fusion(f32[256,128]{1,0:T(8,128)S(1)} %fusion.6, f32[128]{0:T(128)S(1)} %add_rsqrt_fusion, f32[256,128]{1,0:T(8,128)S(1)} %convolution_bitcast_fusion, f32[1,8,2,64,128]{4,3,1,2,0:T(8,128)S(1)} %all_to_all.47, ...), kind=kOutput, calls=%fused_computation.36 | convolution fusion | flops 201555840 | bytes 1311744 | tf_op jit(solution)/shard_map/vmap(snk,snx->kx)/dot_general | solution.py:30
  58.4 31.6 %psum.7 = f32[128]{0:T(128)S(1)} all-reduce(f32[128]{0:T(128)S(1)} %get-tuple-element.3), channel_id=1, replica_groups=mesh['groups'=2,'range'=8,'sub'=2] {'range','sub'}, use_global_device_ids=true, to_apply=%region_2.3 | all-reduce | flops 128 | bytes 1024 | tf_op jit(solution)/shard_map/psum | solution.py:73
  90.1 0.5 broadcast_multiply_fusion.2
  90.7 0.1 copy.31
  90.8 0.8 pad_maximum_fusion
  91.7 0.8 pad_maximum_fusion.1
  (18 shorter events, 0.5 us)
Async XLA Ops:
  0.6 6.0 %copy-start = (f32[2,32,32,128]{3,2,1,0:T(8,128)S(1)}, f32[2,32,32,128]{3,2,1,0:T(8,128)}, u32[]{:S(2)}) copy-start(f32[2,32,32,128]{3,2,1,0:T(8,128)} %param.4) | copy-start | bytes 3145732
  3.2 5.2 %all-to-all-start.2 = ((f32[2,1,65536]{2,1,0:T(1,128)}), f32[2,1,65536]{2,1,0:T(1,128)S(1)}, u32[]{:S(2)}, u32[]{:S(2)}) async-start(f32[2,1,65536]{2,1,0:T(1,128)} %reshape.157), calls=%async_computation.2 | async-start | bytes 1048576 | tf_op jit(solution)/shard_map/all_to_all | solution.py:63
  8.2 7.6 %copy-start.2 = (s32[2]{0:T(128)S(1)}, s32[2]{0:T(128)}, u32[]{:S(2)}) copy-start(s32[2]{0:T(128)} %param.7) | copy-start | bytes 28
  8.4 7.4 %copy-start.1 = (s32[1,8,64]{2,1,0:T(8,128)S(1)}, s32[1,8,64]{2,1,0:T(8,128)}, u32[]{:S(2)}) copy-start(s32[1,8,64]{2,1,0:T(8,128)} %param.6) | copy-start | bytes 6148
  8.4 33.7 %all-to-all-start = ((f32[2,1,1,32,8,2,2,128]{7,6,3,5,0,2,1,4:T(2,128)}), f32[2,1,1,32,8,2,2,128]{7,6,3,5,0,2,1,4:T(2,128)S(1)}, u32[]{:S(2)}, u32[]{:S(2)}) async-start(f32[2,1,1,32,8,2,2,128]{7,6,3,5,0,2,1,4:T(2,128)} %copy.24), calls=%async_computation | async-start | bytes 2097152 | tf_op jit(solution)/shard_map/all_to_all | solution.py:56
where the time goes:
time: 92.9 us; the launch traced here: 92.5 us
  blocking collectives  36.2 us (39%)
  waiting for transfers between devices  19.1 us (21%)
  local copies, waits for them, and re-layouts  12.7 us (14%)
  starting transfers between devices  10.9 us (12%)
  matrix products  8.13 us (9%)
  other arithmetic  4.67 us (5%)
    psum x1, blocking collectives, body(): total = lax.psum(jnp.sum(energies, axis=0), ('range', 'sub'))  31.6 us
    all_to_all x1, waiting for transfers between devices, body(): lax.all_to_all(spread, 'range', split_axis=4, concat_axis=1, tiled=True)  18.9 us
    all_to_all x1, starting transfers between devices, body(): lax.all_to_all(spread, 'range', split_axis=4, concat_axis=1, tiled=True)  7.41 us
    all_to_all x1, blocking collectives, body(): lax.all_to_all(lax.all_to_all(spread, 'range', split_axis=4, concat_axis=...  4.58 us
    all_to_all x3, local copies, waits for them, and re-layouts, body(): lax.all_to_all(beam_weights, 'sub', split_axis=0, concat_axis=4, tiled=True)  4.18 us
    all_to_all x1, starting transfers between devices, body(): lax.all_to_all(beam_weights, 'sub', split_axis=0, concat_axis=4, tiled=True)  3.49 us
    unnamed x8, local copies, waits for them, and re-layouts  3.15 us
    gather x4, local copies, waits for them, and re-layouts, block_terms(): picked = jnp.take(snaps, chosen, axis=1)  2.5 us
  transfers between devices with their start and end apart: 2, of which 2 were waited for; matrix products, arithmetic and copies ran while one was open for 8% of the time, Pallas kernels for 0%

commit v1 on v0

--- a/solution.py
+++ b/solution.py
@@ -70,7 +70,7 @@
     beams = filts.shape[2]
     filtered = filts.reshape(blocks_dev, parts_iq, beams, GB, pulses).transpose(1, 2, 0, 3, 4)
     filtered = filtered.reshape(parts_iq, beams, gate_dev, pulses)
-    total = lax.psum(jnp.sum(energies, axis=0), ("range", "sub"))
+    total = jnp.sum(lax.all_gather(jnp.sum(energies, axis=0), ("range", "sub")), axis=0)
     energy = total / (all_gates * pulses)
     return (covs, filtered, energy)
 

time: 92.9 us -> 80.7 us (0.87)
  blocking collectives: 36.2 us -> 24 us
    psum x1 -> x0, blocking collectives: 31.6 us -> none  [body(): total = lax.psum(jnp.sum(energies, axis=0), ('range', 'sub'))]
    all_gather x0 -> x1, blocking collectives: none -> 19.5 us  [body(): lax.all_gather(jnp.sum(energies, axis=0), ('range', 'sub'))]
  transfers between devices with their start and end apart: 2 -> 2, of which waited for: 2 -> 2; matrix products, arithmetic and copies ran while one was open for 8% -> 9% of each run, Pallas kernels for 0% -> 0%
where the time goes in v1:
time: 80.7 us; the launch traced here: 80.3 us
  blocking collectives  24 us (30%)
  waiting for transfers between devices  19.1 us (24%)
  local copies, waits for them, and re-layouts  12.7 us (16%)
  starting transfers between devices  10.9 us (14%)
  matrix products  8.13 us (10%)
  other arithmetic  4.7 us (6%)
  between operations  0.84 us (1%)
    all_gather x1, blocking collectives, body(): lax.all_gather(jnp.sum(energies, axis=0), ('range', 'sub'))  19.5 us
    all_to_all x1, waiting for transfers between devices, body(): lax.all_to_all(spread, 'range', split_axis=4, concat_axis=1, tiled=True)  18.9 us
    all_to_all x1, starting transfers between devices, body(): lax.all_to_all(spread, 'range', split_axis=4, concat_axis=1, tiled=True)  7.41 us
    all_to_all x1, blocking collectives, body(): lax.all_to_all(lax.all_to_all(spread, 'range', split_axis=4, concat_axis=...  4.58 us
    all_to_all x3, local copies, waits for them, and re-layouts, body(): lax.all_to_all(beam_weights, 'sub', split_axis=0, concat_axis=4, tiled=True)  4.18 us
    all_to_all x1, starting transfers between devices, body(): lax.all_to_all(beam_weights, 'sub', split_axis=0, concat_axis=4, tiled=True)  3.49 us
    unnamed x8, local copies, waits for them, and re-layouts  3.15 us
    gather x4, local copies, waits for them, and re-layouts, block_terms(): picked = jnp.take(snaps, chosen, axis=1)  2.5 us
  transfers between devices with their start and end apart: 2, of which 2 were waited for; matrix products, arithmetic and copies ran while one was open for 9% of the time, Pallas kernels for 0%

profile of v1, /device:TPU:0, one launch (start us, length us, event | category | flops | bytes accessed | tf_op | source)
XLA Modules:
  0.0 80.3 jit_solution(303801115158308347)
XLA Ops:
  0.6 2.5 %reshape.161 = f32[2,1,65536]{2,1,0:T(1,128)} reshape(f32[2,8,2,64,64]{4,3,2,1,0:T(8,128)} %param.5) | data formatting | bytes 1048576
  3.2 3.5 %all-to-all-start.2 = ((f32[2,1,65536]{2,1,0:T(1,128)}), f32[2,1,65536]{2,1,0:T(1,128)S(1)}, u32[]{:S(2)}, u32[]{:S(2)}) async-start(f32[2,1,65536]{2,1,0:T(1,128)} %reshape.161), calls=%async_computation.2 | async-start | bytes 1048576 | tf_op jit(solution)/shard_map/all_to_all | solution.py:63
  6.7 1.6 %copy.24 = f32[2,1,1,32,8,2,2,128]{7,6,3,5,0,2,1,4:T(2,128)} copy(f32[2,1,1,32,8,2,2,128]{7,6,5,4,3,0,2,1:T(2,128)S(1)} %bitcast.104) | data formatting | bytes 2097152 | tf_op jit(solution)/shard_map/reshape | solution.py:54
  8.2 0.2 all-to-all-done.2
  8.4 7.4 %all-to-all-start = ((f32[2,1,1,32,8,2,2,128]{7,6,3,5,0,2,1,4:T(2,128)}), f32[2,1,1,32,8,2,2,128]{7,6,3,5,0,2,1,4:T(2,128)S(1)}, u32[]{:S(2)}, u32[]{:S(2)}) async-start(f32[2,1,1,32,8,2,2,128]{7,6,3,5,0,2,1,4:T(2,128)} %copy.24), calls=%async_computation | async-start | bytes 2097152 | tf_op jit(solution)/shard_map/all_to_all | solution.py:56
  15.9 0.5 broadcast.75
  16.4 2.3 %reduce.6 = f32[2,65536]{1,0:T(2,128)S(1)} reduce(f32[2,1,65536]{2,1,0:T(1,128)S(1)} %all-to-all-done.2, f32[]{:T(128)} %broadcast.75), dimensions={1}, to_apply=%all_to_all.44.reduce_sub_computation | reduce | bytes 1048580 | tf_op jit(solution)/shard_map/all_to_all | solution.py:63
  18.8 0.6 reshape.162
  19.4 1.9 %copy.29 = f32[1,8,2,64,2,64]{5,4,3,1,2,0:T(2,128)} copy(f32[1,8,2,64,2,64]{5,3,2,1,4,0:T(8,128)S(1)} %bitcast.99) | data formatting | bytes 1048576 | tf_op jit(solution)/shard_map/all_to_all | solution.py:63
  21.2 1.8 %all_to_all.47 = f32[1,8,2,64,128]{4,3,1,2,0:T(8,128)S(1)} reshape(f32[1,8,2,64,2,64]{5,4,3,1,2,0:T(2,128)} %copy.29) | data formatting | bytes 1048576 | tf_op jit(solution)/shard_map/all_to_all | solution.py:63
  23.1 18.9 %all-to-all-done = f32[2,1,1,32,8,2,2,128]{7,6,3,5,0,2,1,4:T(2,128)S(1)} async-done(((f32[2,1,1,32,8,2,2,128]{7,6,3,5,0,2,1,4:T(2,128)}), f32[2,1,1,32,8,2,2,128]{7,6,3,5,0,2,1,4:T(2,128)S(1)}, u32[]{:S(2)}, u32[]{:S(2)}) %all-to-all-start) | async-done | bytes 1048608 | tf_op jit(solution)/shard_map/all_to_all | solution.py:56
  42.1 4.6 %all_to_all.51 = f32[2,8,1,32,1,2,2,128]{7,6,3,1,0,4,2,5:T(2,128)S(1)} all-to-all(f32[2,8,1,32,1,2,2,128]{7,6,3,1,0,4,2,5:T(2,128)S(1)} %copy.25), channel_id=1, replica_groups=mesh['groups'=2,'range'=8,'sub'=2] {'sub'}, dimensions={5} | all-to-all | bytes 2097152 | tf_op jit(solution)/shard_map/all_to_all | solution.py:55
  46.8 0.8 %copy.27 = f32[1,2,512,256]{3,1,2,0:T(2,128)S(1)} copy(f32[1,2,512,256]{3,0,2,1:T(1,128)S(1)} %bitcast.101) | data formatting | bytes 2097152 | tf_op jit(solution)/shard_map/transpose;reshape | solution.py:62
  47.6 2.3 %gather_fusion = f32[512,2,256]{2,1,0:T(2,128)S(1)} fusion(f32[1,2,512,256]{3,1,2,0:T(2,128)S(1)} %copy.27, s32[512]{0:T(512)S(1)} %reshape.147), kind=kCustom, calls=%fused_computation | custom fusion | bytes 2101248 | tf_op jit(solution)/shard_map/vmap(jit(_take))/gather | solution.py:12
  50.1 0.1 broadcast_select_fusion
  50.2 1.0 %convolution_bitcast_fusion.2 = f32[256,128]{1,0:T(8,128)S(1)} fusion(f32[1,2,8,64,256]{4,3,2,1,0:T(8,128)S(1)} %broadcast_select_fusion, f32[1,8,2,64,128]{4,3,1,2,0:T(8,128)S(1)} %all_to_all.47), kind=kOutput, calls=%fused_computation.13 | convolution fusion | flops 201326592 | bytes 917504 | tf_op jit(solution)/shard_map/vmap(snk,snx->kx)/dot_general | solution.py:27
  51.2 1.0 %convolution_bitcast_fusion = f32[256,128]{1,0:T(8,128)S(1)} fusion(f32[1,2,8,64,256]{4,3,2,1,0:T(8,128)S(1)} %broadcast_select_fusion, f32[1,8,2,64,128]{4,3,1,2,0:T(8,128)S(1)} %all_to_all.47), kind=kOutput, calls=%fused_computation.11 | convolution fusion | flops 201326592 | bytes 917504 | tf_op jit(solution)/shard_map/vmap(snk,snx->kx)/dot_general | solution.py:30
  52.2 0.6 fusion.12
  52.9 0.6 fusion.2
  53.5 0.4 fusion.19
  53.9 0.4 fusion.18
  54.3 0.6 fusion.8
  54.9 1.0 %fusion.6 = f32[256,128]{1,0:T(8,128)S(1)} fusion(f32[256,128]{1,0:T(8,128)S(1)} %convolution_bitcast_fusion.2, f32[1,2,8,64,256]{4,3,2,1,0:T(8,128)S(1)} %broadcast_select_fusion, f32[1,8,2,64,128]{4,3,1,2,0:T(8,128)S(1)} %all_to_all.47), kind=kOutput, calls=%fused_computation.15 | convolution fusion | flops 201359360 | bytes 1048576 | tf_op jit(solution)/shard_map/vmap(snk,snx->kx)/dot_general | solution.py:27
  55.9 0.6 fusion.3
  56.5 0.4 fusion
  56.9 0.4 fusion.5
  57.4 1.0 %add_reduce_fusion = (f32[128]{0:T(128)S(1)}, f32[256,128]{1,0:T(8,128)S(1)}, f32[256,128]{1,0:T(8,128)S(1)}) fusion(f32[256,128]{1,0:T(8,128)S(1)} %fusion.6, f32[128]{0:T(128)S(1)} %add_rsqrt_fusion, f32[256,128]{1,0:T(8,128)S(1)} %convolution_bitcast_fusion, f32[1,8,2,64,128]{4,3,1,2,0:T(8,128)S(1)} %all_to_all.47, ...), kind=kOutput, calls=%fused_computation.36 | convolution fusion | flops 201555840 | bytes 1311744 | tf_op jit(solution)/shard_map/vmap(snk,snx->kx)/dot_general | solution.py:30
  58.4 0.1 copy.30
  58.5 19.5 %all-gather.1 = f32[16,1,128]{2,1,0:T(1,128)S(1)} all-gather(f32[1,1,128]{2,1,0:T(1,128)S(1)} %bitcast.107), channel_id=2, replica_groups=mesh['groups'=2,'range'=8,'sub'=2] {'range','sub'}, dimensions={0}, use_global_device_ids=true | all-gather | bytes 8704 | tf_op jit(solution)/shard_map/all_gather | solution.py:73
  78.0 0.5 broadcast_multiply_fusion.2
  78.7 0.8 %pad_maximum_fusion = f32[1,8,64,128]{3,2,1,0:T(8,128)} fusion(f32[1,8,64,64]{3,2,1,0:T(8,128)S(1)} %bitcast.103, f32[1,8,64,64]{3,2,1,0:T(8,128)S(1)} %bitcast.97), kind=kLoop, calls=%fused_computation.28 | loop fusion | flops 65536 | bytes 524288 | tf_op jit(solution)/shard_map/vmap()/concatenate | solution.py:43
  79.5 0.8 %pad_maximum_fusion.1 = f32[2,128,2,128]{3,2,1,0:T(2,128)} fusion(f32[1,128,2,128]{3,2,1,0:T(2,128)S(1)} %copy.31, f32[1,128,2,128]{3,2,1,0:T(2,128)S(1)} %copy.30), kind=kLoop, calls=%fused_computation.29 | loop fusion | flops 65536 | bytes 524288 | tf_op jit(solution)/shard_map/vmap()/stack | solution.py:41
  (19 shorter events, 0.6 us)
Async XLA Ops:
  0.6 6.0 %copy-start = (f32[2,32,32,128]{3,2,1,0:T(8,128)S(1)}, f32[2,32,32,128]{3,2,1,0:T(8,128)}, u32[]{:S(2)}) copy-start(f32[2,32,32,128]{3,2,1,0:T(8,128)} %param.4) | copy-start | bytes 3145732
  3.2 5.2 %all-to-all-start.2 = ((f32[2,1,65536]{2,1,0:T(1,128)}), f32[2,1,65536]{2,1,0:T(1,128)S(1)}, u32[]{:S(2)}, u32[]{:S(2)}) async-start(f32[2,1,65536]{2,1,0:T(1,128)} %reshape.161), calls=%async_computation.2 | async-start | bytes 1048576 | tf_op jit(solution)/shard_map/all_to_all | solution.py:63
  8.2 7.6 %copy-start.2 = (s32[2]{0:T(128)S(1)}, s32[2]{0:T(128)}, u32[]{:S(2)}) copy-start(s32[2]{0:T(128)} %param.7) | copy-start | bytes 28
  8.4 7.4 %copy-start.1 = (s32[1,8,64]{2,1,0:T(8,128)S(1)}, s32[1,8,64]{2,1,0:T(8,128)}, u32[]{:S(2)}) copy-start(s32[1,8,64]{2,1,0:T(8,128)} %param.6) | copy-start | bytes 6148
  8.4 33.7 %all-to-all-start = ((f32[2,1,1,32,8,2,2,128]{7,6,3,5,0,2,1,4:T(2,128)}), f32[2,1,1,32,8,2,2,128]{7,6,3,5,0,2,1,4:T(2,128)S(1)}, u32[]{:S(2)}, u32[]{:S(2)}) async-start(f32[2,1,1,32,8,2,2,128]{7,6,3,5,0,2,1,4:T(2,128)} %copy.24), calls=%async_computation | async-start | bytes 2097152 | tf_op jit(solution)/shard_map/all_to_all | solution.py:56
